TPU v7x, 32 devices: a whole 2x2x4 slice. The times are simulated.
32 devices in a mesh: groups: 2 (over y), axial: 16 (over z, x, core).
Axes of the slice: x: 2, y: 2, z: 4, core: 2. Of those that a mesh axis runs over, the one named last changes fastest.
Arguments:
- pair_rep: bfloat16 [192, 96, 128], P(('groups', 'axial')), parts along dimension 0, may hold values from -6 to 6
- norm_out: float32 [128], replicated, may hold values from 0.5 to 1.5
- proj_out: bfloat16 [128, 512], replicated, may hold values from -0.5 to 0.5
- gate_out: bfloat16 [128, 128], replicated, may hold values from -0.5 to 0.5
- mid_out: float32 [128], replicated, may hold values from 0.5 to 1.5
- final_out: bfloat16 [128, 128], replicated, may hold values from -0.5 to 0.5
- norm_in: float32 [128], replicated, may hold values from 0.5 to 1.5
- proj_in: bfloat16 [128, 512], replicated, may hold values from -0.5 to 0.5
- gate_in: bfloat16 [128, 128], replicated, may hold values from -0.5 to 0.5
- mid_in: float32 [128], replicated, may hold values from 0.5 to 1.5
- final_in: bfloat16 [128, 128], replicated, may hold values from -0.5 to 0.5
Outputs:
- updated: bfloat16 [192, 96, 128], P(('groups', 'axial')), parts along dimension 0
There are 2 independent parts, one for each index of `groups`. A program takes and returns all parts, laid end to end along the dimension named above; an argument that names none is the same for every part. Nothing has to cross between parts.
All inputs are finite; a program needn't handle non-finite values.
Results may differ from a plain program's by a relative error of at most 0.013.
Values may be sent and summed in bfloat16 or wider, within the bound.
A program may use at most 64 MiB of HBM per device.

v0:
```python
import jax
import jax.numpy as jnp
from jax import lax
from jax.sharding import PartitionSpec as P

EPS = 1e-05


def normalize(values, gain, axis):
    average = jnp.mean(values, axis=axis, keepdims=True)
    spread = jnp.mean(jnp.square(values - average), axis=axis, keepdims=True)
    return (values - average) * lax.rsqrt(spread + EPS) * gain


def channel_product(left_side, right_side, outgoing):
    formula = "kil,kjl->kij" if outgoing else "kli,klj->kij"
    got_left, got_right = (
        lax.all_to_all(left_side, "axial", split_axis=0, concat_axis=1, tiled=True),
        lax.all_to_all(right_side, "axial", split_axis=0, concat_axis=1, tiled=True),
    )
    return jnp.einsum(formula, got_left, got_right, preferred_element_type=jnp.float32)


def update(pair_rep, norm_gain, weights, gate_weight, mid_gain, final_weight, outgoing):
    normed = normalize(pair_rep.astype(jnp.float32), norm_gain, -1).astype(jnp.bfloat16)
    projected = jnp.einsum("rnc,ck->krn", normed, weights, preferred_element_type=jnp.float32)
    hidden = weights.shape[1] // 4
    left_side = (jax.nn.sigmoid(projected[hidden : 2 * hidden]) * projected[:hidden]).astype(
        jnp.bfloat16
    )
    right_side = (
        jax.nn.sigmoid(projected[3 * hidden :]) * projected[2 * hidden : 3 * hidden]
    ).astype(jnp.bfloat16)
    product = channel_product(left_side, right_side, outgoing)
    tri = lax.all_to_all(
        product.astype(jnp.bfloat16), "axial", split_axis=1, concat_axis=0, tiled=True
    )
    gating = jax.nn.sigmoid(
        jnp.einsum("rnc,ce->rne", normed, gate_weight, preferred_element_type=jnp.float32)
    )
    tri_normed = normalize(tri.astype(jnp.float32), mid_gain[:, None, None], 0).astype(jnp.bfloat16)
    result = jnp.einsum("krn,kc->rnc", tri_normed, final_weight, preferred_element_type=jnp.float32)
    return (pair_rep.astype(jnp.float32) + gating * result).astype(jnp.bfloat16)


def on_device(
    pair_rep,
    norm_out,
    proj_out,
    gate_out,
    mid_out,
    final_out,
    norm_in,
    proj_in,
    gate_in,
    mid_in,
    final_in,
):
    first = update(pair_rep, norm_out, proj_out, gate_out, mid_out, final_out, True)
    return update(first, norm_in, proj_in, gate_in, mid_in, final_in, False)


def solution(mesh):
    placed = (P(("groups", "axial"), None, None), P(), P(), P(), P(), P(), P(), P(), P(), P(), P())
    return jax.shard_map(
        on_device,
        mesh=mesh,
        in_specs=placed,
        out_specs=P(("groups", "axial"), None, None),
        check_vma=False,
    )
```

profile of v0, /device:TPU:0, one launch (start us, length us, event | category | flops | bytes accessed | tf_op | source)
XLA Modules:
  0.0 93.4 jit_solution(2439038225981949099)
XLA Ops:
  0.0 1.1 %convert_reduce_fusion = f32[6,96]{1,0:T(8,128)S(1)} fusion(bf16[6,96,128]{2,1,0:T(8,128)(2,1)} %param.11), kind=kLoop, calls=%fused_computation.20 | loop fusion | flops 146880 | bytes 149760 | tf_op jit(solution)/shard_map/reduce_sum | solution.py:10
  1.1 1.2 %fusion.19 = f32[6,96]{1,0:T(8,128)S(1)} fusion(bf16[6,96,128]{2,1,0:T(8,128)(2,1)} %param.11, f32[6,96]{1,0:T(8,128)S(1)} %broadcast_multiply_fusion.3), kind=kLoop, calls=%fused_computation.35 | loop fusion | flops 294336 | bytes 152064 | tf_op jit(solution)/shard_map/reduce_sum | solution.py:11
  2.3 1.3 %convolution_bitcast_fusion.1 = f32[512,6,96]{0,2,1:T(8,128)S(1)} fusion(bf16[128,512]{1,0:T(8,128)(2,1)S(1)} %copy-done, bf16[6,96,128]{2,1,0:T(8,128)(2,1)} %param.11, f32[128]{0:T(128)} %param.12, f32[6,96]{1,0:T(8,128)S(1)} %add_rsqrt_fusion.3, f32[6,96]{1,0:T(8,128)S(1)} %broadcast_multiply_fusion.3), kind=kOutput, calls=%fused_computation.1 | convolution fusion | flops 75866112 | bytes 1463296 | tf_op jit(solution)/shard_map/rnc,ck->krn/dot_general | solution.py:26
  3.8 0.9 copy.39
  4.6 7.4 %all-to-all-start.1 = ((bf16[128,6,96]{2,1,0:T(8,128)(2,1)}), bf16[128,6,96]{2,1,0:T(8,128)(2,1)S(1)}, u32[]{:S(2)}, u32[]{:S(2)}) async-start(bf16[128,6,96]{2,1,0:T(8,128)(2,1)} %copy.39), calls=%async_computation.1 | async-start | bytes 524288 | tf_op jit(solution)/shard_map/all_to_all | solution.py:19
  12.0 0.9 copy.36
  12.9 9.1 %all-to-all-done.1 = bf16[128,6,96]{2,1,0:T(8,128)(2,1)S(1)} async-done(((bf16[128,6,96]{2,1,0:T(8,128)(2,1)}), bf16[128,6,96]{2,1,0:T(8,128)(2,1)S(1)}, u32[]{:S(2)}, u32[]{:S(2)}) %all-to-all-start.1) | async-done | bytes 147488 | tf_op jit(solution)/shard_map/all_to_all | solution.py:19
  22.1 3.5 %all-to-all-start = ((bf16[128,6,96]{2,1,0:T(8,128)(2,1)}), bf16[128,6,96]{2,1,0:T(8,128)(2,1)S(1)}, u32[]{:S(2)}, u32[]{:S(2)}) async-start(bf16[128,6,96]{2,1,0:T(8,128)(2,1)} %copy.36), calls=%async_computation | async-start | bytes 524288 | tf_op jit(solution)/shard_map/all_to_all | solution.py:18
  25.7 9.9 %all-to-all-done = bf16[128,6,96]{2,1,0:T(8,128)(2,1)S(1)} async-done(((bf16[128,6,96]{2,1,0:T(8,128)(2,1)}), bf16[128,6,96]{2,1,0:T(8,128)(2,1)S(1)}, u32[]{:S(2)}, u32[]{:S(2)}) %all-to-all-start) | async-done | bytes 147488 | tf_op jit(solution)/shard_map/all_to_all | solution.py:18
  35.9 0.7 copy.44
  36.6 3.7 %all-to-all-start.2 = ((bf16[8,96,96]{2,0,1:T(8,128)(2,1)}), bf16[8,96,96]{2,0,1:T(8,128)(2,1)S(1)}, u32[]{:S(2)}, u32[]{:S(2)}) async-start(bf16[8,96,96]{2,0,1:T(8,128)(2,1)} %copy.44), calls=%async_computation.2 | async-start | bytes 393216 | tf_op jit(solution)/shard_map/all_to_all | solution.py:35
  40.7 8.5 %all-to-all-done.2 = bf16[8,96,96]{2,0,1:T(8,128)(2,1)S(1)} async-done(((bf16[8,96,96]{2,0,1:T(8,128)(2,1)}), bf16[8,96,96]{2,0,1:T(8,128)(2,1)S(1)}, u32[]{:S(2)}, u32[]{:S(2)}) %all-to-all-start.2) | async-done | bytes 147488 | tf_op jit(solution)/shard_map/all_to_all | solution.py:35
  49.4 0.4 fusion.60
  50.1 0.4 convolution_bitcast_fusion
  50.7 0.9 copy.47
  51.6 3.5 %all-to-all-start.3 = ((bf16[128,6,96]{2,1,0:T(8,128)(2,1)}), bf16[128,6,96]{2,1,0:T(8,128)(2,1)S(1)}, u32[]{:S(2)}, u32[]{:S(2)}) async-start(bf16[128,6,96]{2,1,0:T(8,128)(2,1)} %copy.47), calls=%async_computation.3 | async-start | bytes 524288 | tf_op jit(solution)/shard_map/all_to_all | solution.py:18
  55.1 0.9 copy.50
  56.0 9.1 %all-to-all-done.3 = bf16[128,6,96]{2,1,0:T(8,128)(2,1)S(1)} async-done(((bf16[128,6,96]{2,1,0:T(8,128)(2,1)}), bf16[128,6,96]{2,1,0:T(8,128)(2,1)S(1)}, u32[]{:S(2)}, u32[]{:S(2)}) %all-to-all-start.3) | async-done | bytes 147488 | tf_op jit(solution)/shard_map/all_to_all | solution.py:18
  65.1 3.5 %all-to-all-start.4 = ((bf16[128,6,96]{2,1,0:T(8,128)(2,1)}), bf16[128,6,96]{2,1,0:T(8,128)(2,1)S(1)}, u32[]{:S(2)}, u32[]{:S(2)}) async-start(bf16[128,6,96]{2,1,0:T(8,128)(2,1)} %copy.50), calls=%async_computation.4 | async-start | bytes 524288 | tf_op jit(solution)/shard_map/all_to_all | solution.py:19
  68.7 9.9 %all-to-all-done.4 = bf16[128,6,96]{2,1,0:T(8,128)(2,1)S(1)} async-done(((bf16[128,6,96]{2,1,0:T(8,128)(2,1)}), bf16[128,6,96]{2,1,0:T(8,128)(2,1)S(1)}, u32[]{:S(2)}, u32[]{:S(2)}) %all-to-all-start.4) | async-done | bytes 147488 | tf_op jit(solution)/shard_map/all_to_all | solution.py:19
  78.9 0.7 copy.55
  79.6 3.7 %all-to-all-start.5 = ((bf16[8,96,96]{2,0,1:T(8,128)(2,1)}), bf16[8,96,96]{2,0,1:T(8,128)(2,1)S(1)}, u32[]{:S(2)}, u32[]{:S(2)}) async-start(bf16[8,96,96]{2,0,1:T(8,128)(2,1)} %copy.55), calls=%async_computation.5 | async-start | bytes 393216 | tf_op jit(solution)/shard_map/all_to_all | solution.py:35
  83.7 8.6 %all-to-all-done.5 = bf16[8,96,96]{2,0,1:T(8,128)(2,1)S(1)} async-done(((bf16[8,96,96]{2,0,1:T(8,128)(2,1)}), bf16[8,96,96]{2,0,1:T(8,128)(2,1)S(1)}, u32[]{:S(2)}, u32[]{:S(2)}) %all-to-all-start.5) | async-done | bytes 147488 | tf_op jit(solution)/shard_map/all_to_all | solution.py:35
  92.4 1.0 %fusion.10 = bf16[6,96,128]{2,1,0:T(8,128)(2,1)} fusion(f32[6,96,128]{2,1,0:T(8,128)S(1)} %get-tuple-element.10, f32[6,96,128]{2,1,0:T(8,128)S(1)} %fusion.4, f32[128]{0:T(128)S(1)} %copy-done.6, f32[6,96]{1,0:T(8,128)S(1)} %add_rsqrt_fusion, f32[6,96]{1,0:T(8,128)S(1)} %broadcast_multiply_fusion, bf16[128,128]{1,0:T(8,128)(2,1)S(1)} %copy-done.4, ...), kind=kOutput, calls=%fused_computation.18 | convolution fusion | flops 19464192 | bytes 922624 | tf_op jit(solution)/shard_map/krn,kc->rnc/dot_general | solution.py:42
  (45 shorter events, 2.3 us)
Async XLA Ops:
  0.0 2.3 %copy-start = (bf16[128,512]{1,0:T(8,128)(2,1)S(1)}, bf16[128,512]{1,0:T(8,128)(2,1)}, u32[]{:S(2)}) copy-start(bf16[128,512]{1,0:T(8,128)(2,1)} %param.13) | copy-start | bytes 393220
  4.6 17.4 %all-to-all-start.1 = ((bf16[128,6,96]{2,1,0:T(8,128)(2,1)}), bf16[128,6,96]{2,1,0:T(8,128)(2,1)S(1)}, u32[]{:S(2)}, u32[]{:S(2)}) async-start(bf16[128,6,96]{2,1,0:T(8,128)(2,1)} %copy.39), calls=%async_computation.1 | async-start | bytes 524288 | tf_op jit(solution)/shard_map/all_to_all | solution.py:19
  22.1 13.5 %all-to-all-start = ((bf16[128,6,96]{2,1,0:T(8,128)(2,1)}), bf16[128,6,96]{2,1,0:T(8,128)(2,1)S(1)}, u32[]{:S(2)}, u32[]{:S(2)}) async-start(bf16[128,6,96]{2,1,0:T(8,128)(2,1)} %copy.36), calls=%async_computation | async-start | bytes 524288 | tf_op jit(solution)/shard_map/all_to_all | solution.py:18
  25.6 14.7 %copy-start.1 = (bf16[6,96,128]{2,1,0:T(8,128)(2,1)S(1)}, bf16[6,96,128]{2,1,0:T(8,128)(2,1)}, u32[]{:S(2)}) copy-start(bf16[6,96,128]{2,1,0:T(8,128)(2,1)} %param.11) | copy-start | bytes 442372
  25.6 14.7 %copy-start.7 = (f32[128]{0:T(128)S(1)}, f32[128]{0:T(128)}, u32[]{:S(2)}) copy-start(f32[128]{0:T(128)} %param.12) | copy-start | bytes 1540
  25.6 14.7 %copy-start.9 = (bf16[128,128]{1,0:T(8,128)(2,1)S(1)}, bf16[128,128]{1,0:T(8,128)(2,1)}, u32[]{:S(2)}) copy-start(bf16[128,128]{1,0:T(8,128)(2,1)} %param.14) | copy-start | bytes 98308
  36.6 12.8 %copy-start.3 = (bf16[128,128]{1,0:T(8,128)(2,1)S(1)}, bf16[128,128]{1,0:T(8,128)(2,1)}, u32[]{:S(2)}) copy-start(bf16[128,128]{1,0:T(8,128)(2,1)} %param.16) | copy-start | bytes 98308
  36.6 12.8 %copy-start.5 = (f32[128]{0:T(128)S(1)}, f32[128]{0:T(128)}, u32[]{:S(2)}) copy-start(f32[128]{0:T(128)} %param.15) | copy-start | bytes 1540
  36.6 12.6 %all-to-all-start.2 = ((bf16[8,96,96]{2,0,1:T(8,128)(2,1)}), bf16[8,96,96]{2,0,1:T(8,128)(2,1)S(1)}, u32[]{:S(2)}, u32[]{:S(2)}) async-start(bf16[8,96,96]{2,0,1:T(8,128)(2,1)} %copy.44), calls=%async_computation.2 | async-start | bytes 393216 | tf_op jit(solution)/shard_map/all_to_all | solution.py:35
  40.7 9.5 %copy-start.2 = (bf16[128,512]{1,0:T(8,128)(2,1)S(1)}, bf16[128,512]{1,0:T(8,128)(2,1)}, u32[]{:S(2)}) copy-start(bf16[128,512]{1,0:T(8,128)(2,1)} %param.18) | copy-start | bytes 393220
  40.7 9.5 %copy-start.8 = (f32[128]{0:T(128)S(1)}, f32[128]{0:T(128)}, u32[]{:S(2)}) copy-start(f32[128]{0:T(128)} %param.17) | copy-start | bytes 1540
  51.6 13.5 %all-to-all-start.3 = ((bf16[128,6,96]{2,1,0:T(8,128)(2,1)}), bf16[128,6,96]{2,1,0:T(8,128)(2,1)S(1)}, u32[]{:S(2)}, u32[]{:S(2)}) async-start(bf16[128,6,96]{2,1,0:T(8,128)(2,1)} %copy.47), calls=%async_computation.3 | async-start | bytes 524288 | tf_op jit(solution)/shard_map/all_to_all | solution.py:18
  65.1 13.5 %all-to-all-start.4 = ((bf16[128,6,96]{2,1,0:T(8,128)(2,1)}), bf16[128,6,96]{2,1,0:T(8,128)(2,1)S(1)}, u32[]{:S(2)}, u32[]{:S(2)}) async-start(bf16[128,6,96]{2,1,0:T(8,128)(2,1)} %copy.50), calls=%async_computation.4 | async-start | bytes 524288 | tf_op jit(solution)/shard_map/all_to_all | solution.py:19
  68.6 14.7 %copy-start.10 = (bf16[128,128]{1,0:T(8,128)(2,1)S(1)}, bf16[128,128]{1,0:T(8,128)(2,1)}, u32[]{:S(2)}) copy-start(bf16[128,128]{1,0:T(8,128)(2,1)} %param.19) | copy-start | bytes 98308
  79.6 12.8 %copy-start.4 = (bf16[128,128]{1,0:T(8,128)(2,1)S(1)}, bf16[128,128]{1,0:T(8,128)(2,1)}, u32[]{:S(2)}) copy-start(bf16[128,128]{1,0:T(8,128)(2,1)} %param.21) | copy-start | bytes 98308
  79.6 12.8 %copy-start.6 = (f32[128]{0:T(128)S(1)}, f32[128]{0:T(128)}, u32[]{:S(2)}) copy-start(f32[128]{0:T(128)} %param.20) | copy-start | bytes 1540
  79.6 12.6 %all-to-all-start.5 = ((bf16[8,96,96]{2,0,1:T(8,128)(2,1)}), bf16[8,96,96]{2,0,1:T(8,128)(2,1)S(1)}, u32[]{:S(2)}, u32[]{:S(2)}) async-start(bf16[8,96,96]{2,0,1:T(8,128)(2,1)} %copy.55), calls=%async_computation.5 | async-start | bytes 393216 | tf_op jit(solution)/shard_map/all_to_all | solution.py:35
where the time goes:
time: 94.3 us; the launch traced here: 93.4 us
  waiting for transfers between devices  55.1 us (58%)
  starting transfers between devices  25.3 us (27%)
  local copies, waits for them, and re-layouts  5.17 us (5%)
  matrix products  4.23 us (4%)
  other arithmetic  3.23 us (3%)
    all_to_all x2, waiting for transfers between devices, channel_product(): lax.all_to_all(right_side, 'axial', split_axis=0, concat_axis=1, tiled=True)  19.1 us
    all_to_all x2, waiting for transfers between devices, channel_product(): lax.all_to_all(left_side, 'axial', split_axis=0, concat_axis=1, tiled=True)  19 us
    all_to_all x2, waiting for transfers between devices, update(): lax.all_to_all(product.astype(jnp.bfloat16), 'axial', split_axis=1, conca...  17.1 us
    all_to_all x2, starting transfers between devices, channel_product(): lax.all_to_all(right_side, 'axial', split_axis=0, concat_axis=1, tiled=True)  10.9 us
    all_to_all x2, starting transfers between devices, update(): lax.all_to_all(product.astype(jnp.bfloat16), 'axial', split_axis=1, conca...  7.31 us
    all_to_all x2, starting transfers between devices, channel_product(): lax.all_to_all(left_side, 'axial', split_axis=0, concat_axis=1, tiled=True)  7.06 us
  transfers between devices with their start and end apart: 6, of which 6 were waited for; matrix products, arithmetic and copies ran while one was open for 3% of the time, Pallas kernels for 0%

commit v1 on v0

--- a/solution.py
+++ b/solution.py
@@ -4,6 +4,13 @@
 from jax.sharding import PartitionSpec as P
 
 EPS = 1e-05
+
+
+def stacked_exchange(x, mesh_axis, split, join):
+    size = lax.axis_size(mesh_axis)
+    blocks = jnp.stack(jnp.split(x, size, axis=split), axis=0)
+    blocks = lax.all_to_all(blocks, mesh_axis, split_axis=0, concat_axis=0)
+    return jnp.concatenate(blocks, axis=join)
 
 
 def normalize(values, gain, axis):
@@ -15,7 +22,7 @@
 def channel_product(left_side, right_side, outgoing):
     formula = "kil,kjl->kij" if outgoing else "kli,klj->kij"
     got_left, got_right = (
-        lax.all_to_all(left_side, "axial", split_axis=0, concat_axis=1, tiled=True),
+        stacked_exchange(left_side, "axial", 0, 1),
         lax.all_to_all(right_side, "axial", split_axis=0, concat_axis=1, tiled=True),
     )
     return jnp.einsum(formula, got_left, got_right, preferred_element_type=jnp.float32)

time: 94.3 us -> 101 us (1.071)
  local copies, waits for them, and re-layouts: 5.17 us -> 27.5 us
  waiting for transfers between devices: 55.1 us -> 35.7 us
  starting transfers between devices: 25.3 us -> 29.5 us
    all_to_all x2, waiting for transfers between devices: 19.1 us -> 0.75 us  [channel_product(): lax.all_to_all(right_side, 'axial', split_axis=0, concat_axis=1, tiled=True)]
    unnamed x22 -> x52, local copies, waits for them, and re-layouts: 0.06 us -> 18.1 us
    another operation x0 -> x36, local copies, waits for them, and re-layouts: none -> 6 us  [stacked_exchange(): blocks = jnp.stack(jnp.split(x, size, axis=split), axis=0)]
    all_to_all x2, starting transfers between devices: 7.06 us -> 11.2 us  [stacked_exchange(): blocks = lax.all_to_all(blocks, mesh_axis, split_axis=0, concat_axis=0)]
    convert_element_type x2 -> x0, local copies, waits for them, and re-layouts: 1.77 us -> none  [update(): (jax.nn.sigmoid(projected[hidden:2 * hidden]) * projected[:hidden]).astyp...]
    all_to_all x2, waiting for transfers between devices: 19 us -> 17.8 us  [stacked_exchange(): blocks = lax.all_to_all(blocks, mesh_axis, split_axis=0, concat_axis=0)]
  transfers between devices with their start and end apart: 6 -> 6, of which waited for: 6 -> 5; matrix products, arithmetic and copies ran while one was open for 3% -> 22% of each run, Pallas kernels for 0% -> 0%
where the time goes in v1:
time: 101 us; the launch traced here: 100 us
  waiting for transfers between devices  35.7 us (35%)
  starting transfers between devices  29.5 us (29%)
  local copies, waits for them, and re-layouts  27.5 us (27%)
  matrix products  4.23 us (4%)
  other arithmetic  3.23 us (3%)
    unnamed x52, local copies, waits for them, and re-layouts  18.1 us
    all_to_all x2, waiting for transfers between devices, stacked_exchange(): blocks = lax.all_to_all(blocks, mesh_axis, split_axis=0, concat_axis=0)  17.8 us
    all_to_all x2, waiting for transfers between devices, update(): lax.all_to_all(product.astype(jnp.bfloat16), 'axial', split_axis=1, conca...  17.1 us
    all_to_all x2, starting transfers between devices, stacked_exchange(): blocks = lax.all_to_all(blocks, mesh_axis, split_axis=0, concat_axis=0)  11.2 us
    all_to_all x2, starting transfers between devices, channel_product(): lax.all_to_all(right_side, 'axial', split_axis=0, concat_axis=1, tiled=True)  10.9 us
    all_to_all x2, starting transfers between devices, update(): lax.all_to_all(product.astype(jnp.bfloat16), 'axial', split_axis=1, conca...  7.31 us
    another operation x36, local copies, waits for them, and re-layouts, stacked_exchange(): blocks = jnp.stack(jnp.split(x, size, axis=split), axis=0)  6 us
  transfers between devices with their start and end apart: 6, of which 5 were waited for; matrix products, arithmetic and copies ran while one was open for 22% of the time, Pallas kernels for 0%

profile of v1, /device:TPU:0, one launch (start us, length us, event | category | flops | bytes accessed | tf_op | source)
XLA Modules:
  0.0 100.4 jit_solution(4192014433502394137)
XLA Ops:
  0.0 1.1 %convert_reduce_fusion = f32[6,96]{1,0:T(8,128)S(1)} fusion(bf16[6,96,128]{2,1,0:T(8,128)(2,1)} %param.11), kind=kLoop, calls=%fused_computation.20 | loop fusion | flops 146880 | bytes 149760 | tf_op jit(solution)/shard_map/reduce_sum | solution.py:17
  1.1 1.2 %fusion.19 = f32[6,96]{1,0:T(8,128)S(1)} fusion(bf16[6,96,128]{2,1,0:T(8,128)(2,1)} %param.11, f32[6,96]{1,0:T(8,128)S(1)} %broadcast_multiply_fusion.3), kind=kLoop, calls=%fused_computation.35 | loop fusion | flops 294336 | bytes 152064 | tf_op jit(solution)/shard_map/reduce_sum | solution.py:18
  2.3 1.3 %convolution_bitcast_fusion.1 = f32[512,6,96]{0,2,1:T(8,128)S(1)} fusion(bf16[128,512]{1,0:T(8,128)(2,1)S(1)} %copy-done, bf16[6,96,128]{2,1,0:T(8,128)(2,1)} %param.11, f32[128]{0:T(128)} %param.12, f32[6,96]{1,0:T(8,128)S(1)} %add_rsqrt_fusion.3, f32[6,96]{1,0:T(8,128)S(1)} %broadcast_multiply_fusion.3), kind=kOutput, calls=%fused_computation.1 | convolution fusion | flops 75866112 | bytes 1463296 | tf_op jit(solution)/shard_map/rnc,ck->krn/dot_general | solution.py:33
  3.8 0.9 copy.96
  4.6 7.4 %all-to-all-start.1 = ((bf16[128,6,96]{2,1,0:T(8,128)(2,1)}), bf16[128,6,96]{2,1,0:T(8,128)(2,1)S(1)}, u32[]{:S(2)}, u32[]{:S(2)}) async-start(bf16[128,6,96]{2,1,0:T(8,128)(2,1)} %copy.96), calls=%async_computation.1 | async-start | bytes 524288 | tf_op jit(solution)/shard_map/all_to_all | solution.py:26
  12.0 0.6 slice_bitcast_fusion.16
  14.9 0.6 constant_dynamic-update-slice_fusion.14
  24.1 6.0 %all-to-all-start = ((bf16[16,8,6,96]{3,1,2,0:T(8,128)(2,1)}), bf16[16,8,6,96]{3,1,2,0:T(8,128)(2,1)S(1)}, u32[]{:S(2)}, u32[]{:S(2)}) async-start(bf16[16,8,6,96]{3,1,2,0:T(8,128)(2,1)} %constant_dynamic-update-slice_fusion), calls=%async_computation | async-start | bytes 393216 | tf_op jit(solution)/shard_map/all_to_all | solution.py:12
  30.2 8.9 %all-to-all-done = bf16[16,8,6,96]{3,1,2,0:T(8,128)(2,1)S(1)} async-done(((bf16[16,8,6,96]{3,1,2,0:T(8,128)(2,1)}), bf16[16,8,6,96]{3,1,2,0:T(8,128)(2,1)S(1)}, u32[]{:S(2)}, u32[]{:S(2)}) %all-to-all-start) | async-done | bytes 147488 | tf_op jit(solution)/shard_map/all_to_all | solution.py:12
  39.4 0.8 copy.101
  40.1 3.7 %all-to-all-start.2 = ((bf16[8,96,96]{2,0,1:T(8,128)(2,1)}), bf16[8,96,96]{2,0,1:T(8,128)(2,1)S(1)}, u32[]{:S(2)}, u32[]{:S(2)}) async-start(bf16[8,96,96]{2,0,1:T(8,128)(2,1)} %copy.101), calls=%async_computation.2 | async-start | bytes 393216 | tf_op jit(solution)/shard_map/all_to_all | solution.py:42
  44.2 8.5 %all-to-all-done.2 = bf16[8,96,96]{2,0,1:T(8,128)(2,1)S(1)} async-done(((bf16[8,96,96]{2,0,1:T(8,128)(2,1)}), bf16[8,96,96]{2,0,1:T(8,128)(2,1)S(1)}, u32[]{:S(2)}, u32[]{:S(2)}) %all-to-all-start.2) | async-done | bytes 147488 | tf_op jit(solution)/shard_map/all_to_all | solution.py:42
  54.2 0.6 slice_bitcast_fusion
  55.0 0.6 constant_dynamic-update-slice_fusion.31
  57.1 0.9 copy.120
  57.9 3.5 %all-to-all-start.4 = ((bf16[128,6,96]{2,1,0:T(8,128)(2,1)}), bf16[128,6,96]{2,1,0:T(8,128)(2,1)S(1)}, u32[]{:S(2)}, u32[]{:S(2)}) async-start(bf16[128,6,96]{2,1,0:T(8,128)(2,1)} %copy.120), calls=%async_computation.4 | async-start | bytes 524288 | tf_op jit(solution)/shard_map/all_to_all | solution.py:26
  69.5 0.6 constant_dynamic-update-slice_fusion.17
  70.7 0.7 all-to-all-done.4
  71.5 5.2 %all-to-all-start.3 = ((bf16[16,8,6,96]{3,1,2,0:T(8,128)(2,1)}), bf16[16,8,6,96]{3,1,2,0:T(8,128)(2,1)S(1)}, u32[]{:S(2)}, u32[]{:S(2)}) async-start(bf16[16,8,6,96]{3,1,2,0:T(8,128)(2,1)} %constant_dynamic-update-slice_fusion.16), calls=%async_computation.3 | async-start | bytes 393216 | tf_op jit(solution)/shard_map/all_to_all | solution.py:12
  76.7 8.9 %all-to-all-done.3 = bf16[16,8,6,96]{3,1,2,0:T(8,128)(2,1)S(1)} async-done(((bf16[16,8,6,96]{3,1,2,0:T(8,128)(2,1)}), bf16[16,8,6,96]{3,1,2,0:T(8,128)(2,1)S(1)}, u32[]{:S(2)}, u32[]{:S(2)}) %all-to-all-start.3) | async-done | bytes 147488 | tf_op jit(solution)/shard_map/all_to_all | solution.py:12
  85.9 0.8 copy.125
  86.7 3.7 %all-to-all-start.5 = ((bf16[8,96,96]{2,0,1:T(8,128)(2,1)}), bf16[8,96,96]{2,0,1:T(8,128)(2,1)S(1)}, u32[]{:S(2)}, u32[]{:S(2)}) async-start(bf16[8,96,96]{2,0,1:T(8,128)(2,1)} %copy.125), calls=%async_computation.5 | async-start | bytes 393216 | tf_op jit(solution)/shard_map/all_to_all | solution.py:42
  90.7 8.6 %all-to-all-done.5 = bf16[8,96,96]{2,0,1:T(8,128)(2,1)S(1)} async-done(((bf16[8,96,96]{2,0,1:T(8,128)(2,1)}), bf16[8,96,96]{2,0,1:T(8,128)(2,1)S(1)}, u32[]{:S(2)}, u32[]{:S(2)}) %all-to-all-start.5) | async-done | bytes 147488 | tf_op jit(solution)/shard_map/all_to_all | solution.py:42
  99.4 1.0 fusion.10
  (107 shorter events, 24.0 us)
Async XLA Ops:
  0.0 2.3 %copy-start = (bf16[128,512]{1,0:T(8,128)(2,1)S(1)}, bf16[128,512]{1,0:T(8,128)(2,1)}, u32[]{:S(2)}) copy-start(bf16[128,512]{1,0:T(8,128)(2,1)} %param.13) | copy-start | bytes 393220
  4.6 19.5 %all-to-all-start.1 = ((bf16[128,6,96]{2,1,0:T(8,128)(2,1)}), bf16[128,6,96]{2,1,0:T(8,128)(2,1)S(1)}, u32[]{:S(2)}, u32[]{:S(2)}) async-start(bf16[128,6,96]{2,1,0:T(8,128)(2,1)} %copy.96), calls=%async_computation.1 | async-start | bytes 524288 | tf_op jit(solution)/shard_map/all_to_all | solution.py:26
  22.9 20.9 %copy-start.1 = (bf16[6,96,128]{2,1,0:T(8,128)(2,1)S(1)}, bf16[6,96,128]{2,1,0:T(8,128)(2,1)}, u32[]{:S(2)}) copy-start(bf16[6,96,128]{2,1,0:T(8,128)(2,1)} %param.11) | copy-start | bytes 442372
  22.9 20.9 %copy-start.7 = (f32[128]{0:T(128)S(1)}, f32[128]{0:T(128)}, u32[]{:S(2)}) copy-start(f32[128]{0:T(128)} %param.12) | copy-start | bytes 1540
  22.9 20.9 %copy-start.9 = (bf16[128,128]{1,0:T(8,128)(2,1)S(1)}, bf16[128,128]{1,0:T(8,128)(2,1)}, u32[]{:S(2)}) copy-start(bf16[128,128]{1,0:T(8,128)(2,1)} %param.14) | copy-start | bytes 98308
  24.1 15.0 %all-to-all-start = ((bf16[16,8,6,96]{3,1,2,0:T(8,128)(2,1)}), bf16[16,8,6,96]{3,1,2,0:T(8,128)(2,1)S(1)}, u32[]{:S(2)}, u32[]{:S(2)}) async-start(bf16[16,8,6,96]{3,1,2,0:T(8,128)(2,1)} %constant_dynamic-update-slice_fusion), calls=%async_computation | async-start | bytes 393216 | tf_op jit(solution)/shard_map/all_to_all | solution.py:12
  40.1 12.8 %copy-start.3 = (bf16[128,128]{1,0:T(8,128)(2,1)S(1)}, bf16[128,128]{1,0:T(8,128)(2,1)}, u32[]{:S(2)}) copy-start(bf16[128,128]{1,0:T(8,128)(2,1)} %param.16) | copy-start | bytes 98308
  40.1 12.8 %copy-start.5 = (f32[128]{0:T(128)S(1)}, f32[128]{0:T(128)}, u32[]{:S(2)}) copy-start(f32[128]{0:T(128)} %param.15) | copy-start | bytes 1540
  40.1 12.6 %all-to-all-start.2 = ((bf16[8,96,96]{2,0,1:T(8,128)(2,1)}), bf16[8,96,96]{2,0,1:T(8,128)(2,1)S(1)}, u32[]{:S(2)}, u32[]{:S(2)}) async-start(bf16[8,96,96]{2,0,1:T(8,128)(2,1)} %copy.101), calls=%async_computation.2 | async-start | bytes 393216 | tf_op jit(solution)/shard_map/all_to_all | solution.py:42
  44.2 9.5 %copy-start.2 = (bf16[128,512]{1,0:T(8,128)(2,1)S(1)}, bf16[128,512]{1,0:T(8,128)(2,1)}, u32[]{:S(2)}) copy-start(bf16[128,512]{1,0:T(8,128)(2,1)} %param.18) | copy-start | bytes 393220
  44.2 9.5 %copy-start.8 = (f32[128]{0:T(128)S(1)}, f32[128]{0:T(128)}, u32[]{:S(2)}) copy-start(f32[128]{0:T(128)} %param.17) | copy-start | bytes 1540
  57.9 13.5 %all-to-all-start.4 = ((bf16[128,6,96]{2,1,0:T(8,128)(2,1)}), bf16[128,6,96]{2,1,0:T(8,128)(2,1)S(1)}, u32[]{:S(2)}, u32[]{:S(2)}) async-start(bf16[128,6,96]{2,1,0:T(8,128)(2,1)} %copy.120), calls=%async_computation.4 | async-start | bytes 524288 | tf_op jit(solution)/shard_map/all_to_all | solution.py:26
  69.5 20.9 %copy-start.10 = (bf16[128,128]{1,0:T(8,128)(2,1)S(1)}, bf16[128,128]{1,0:T(8,128)(2,1)}, u32[]{:S(2)}) copy-start(bf16[128,128]{1,0:T(8,128)(2,1)} %param.19) | copy-start | bytes 98308
  71.5 14.2 %all-to-all-start.3 = ((bf16[16,8,6,96]{3,1,2,0:T(8,128)(2,1)}), bf16[16,8,6,96]{3,1,2,0:T(8,128)(2,1)S(1)}, u32[]{:S(2)}, u32[]{:S(2)}) async-start(bf16[16,8,6,96]{3,1,2,0:T(8,128)(2,1)} %constant_dynamic-update-slice_fusion.16), calls=%async_computation.3 | async-start | bytes 393216 | tf_op jit(solution)/shard_map/all_to_all | solution.py:12
  86.7 12.8 %copy-start.4 = (bf16[128,128]{1,0:T(8,128)(2,1)S(1)}, bf16[128,128]{1,0:T(8,128)(2,1)}, u32[]{:S(2)}) copy-start(bf16[128,128]{1,0:T(8,128)(2,1)} %param.21) | copy-start | bytes 98308
  86.7 12.8 %copy-start.6 = (f32[128]{0:T(128)S(1)}, f32[128]{0:T(128)}, u32[]{:S(2)}) copy-start(f32[128]{0:T(128)} %param.20) | copy-start | bytes 1540
  86.7 12.6 %all-to-all-start.5 = ((bf16[8,96,96]{2,0,1:T(8,128)(2,1)}), bf16[8,96,96]{2,0,1:T(8,128)(2,1)S(1)}, u32[]{:S(2)}, u32[]{:S(2)}) async-start(bf16[8,96,96]{2,0,1:T(8,128)(2,1)} %copy.125), calls=%async_computation.5 | async-start | bytes 393216 | tf_op jit(solution)/shard_map/all_to_all | solution.py:42
